TPU v7x, 32 devices: a whole 2x2x4 slice. The times are simulated.
32 devices in a mesh: group: 2 (over y), cp: 8 (over z, x), hd: 2 (over core).
Axes of the slice: x: 2, y: 2, z: 4, core: 2. Of those that a mesh axis runs over, the one named last changes fastest.
Arguments:
- doc_lengths: int32 [8], P('group'), parts along dimension 0, may hold values from 1 to 384, 1024 in all
- queries: bfloat16 [2048, 4096], P(('group', 'cp'), 'hd'), parts along dimension 0, may hold values from -52 to 52
- key_states: bfloat16 [2048, 1024], P(('group', 'cp'), 'hd'), parts along dimension 0, may hold values from -4 to 4
- value_head_states: bfloat16 [2048, 1024], P(('group', 'cp'), 'hd'), parts along dimension 0, may hold values from -6 to 6
- out_grad: bfloat16 [2048, 4096], P(('group', 'cp'), 'hd'), parts along dimension 0, may hold values from -6 to 6
Outputs:
- attended: bfloat16 [2048, 4096], P(('group', 'cp'), 'hd'), parts along dimension 0
- grad_queries: bfloat16 [2048, 4096], P(('group', 'cp'), 'hd'), parts along dimension 0
- grad_keys: bfloat16 [2048, 1024], P(('group', 'cp'), 'hd'), parts along dimension 0
- grad_values: bfloat16 [2048, 1024], P(('group', 'cp'), 'hd'), parts along dimension 0
There are 2 independent parts, one for each index of `group`. A program takes and returns all parts, laid end to end along the dimension named above; each array names one. Nothing has to cross between parts.
Inputs may be any that keep to these rules, and one draw needn't show every extreme that they name: `doc_lengths`: documents lie end to end in token order; their lengths sum to 1024.
All inputs are finite; a program needn't handle non-finite values.
Results may differ from a plain program's by a relative error of at most 0.028.
Values may be sent and summed in bfloat16 or wider, within the bound.
A program may use at most 64 MiB of HBM per device.

v0:
```python
import functools
import math

import jax
import jax.numpy as jnp
from jax import lax
from jax.experimental import pallas as pl
from jax.experimental.pallas import tpu as pltpu
from jax.sharding import PartitionSpec as P

HEAD = 128
REACH = 3
MASKED = -1e30
MESH = pl.DeviceIdType.MESH
X, B, T = range(3)


def kernel(
    n, docs, doc_hbm, q_hbm, k_hbm, v_hbm, do_hbm, o_ref, gq_ref, gk_ref, gv_ref,
    kv, qb, db, own, mid, part, back, bias, doc_ref,
    doc_sem, kv_sem, q_sem, fs_sem, fr_sem, bs_sem, br_sem,
):
    tok = q_hbm.shape[0]
    heads = k_hbm.shape[1] // HEAD
    group = q_hbm.shape[1] // k_hbm.shape[1]
    me = lax.axis_index("cp")
    odd = lax.rem(me, 2)
    is_odd = odd == 1
    is_even = odd == 0
    partner = me + 1 - 2 * odd
    own_rows = pl.ds(REACH * tok, tok)

    def rows(dist):
        return pl.ds((REACH - dist) * tok, tok)

    def cols(h):
        return pl.ds(h * HEAD, HEAD)

    doc_load = pltpu.make_async_copy(doc_hbm, doc_ref, doc_sem)
    doc_load.start()
    kv_loads = []
    for g in range(heads):
        kv_loads.append([
            pltpu.make_async_copy(src.at[:, cols(g)], kv.at[g, t, own_rows], kv_sem.at[g, t])
            for t, src in enumerate((k_hbm, v_hbm))
        ])
        for c in kv_loads[g]:
            c.start()
    q_loads = []
    for h in range(heads * group):
        q_loads.append([
            pltpu.make_async_copy(q_hbm.at[:, cols(h)], qb.at[h], q_sem.at[0, h]),
            pltpu.make_async_copy(do_hbm.at[:, cols(h)], db.at[h], q_sem.at[1, h]),
        ])
        for c in q_loads[h]:
            c.start()

    barrier = pltpu.get_barrier_semaphore()
    for to, cond in ((me - 2, me >= 2), (me + 2, me + 2 < n), (partner, me >= 0)):
        @pl.when(cond)
        def _():
            pl.semaphore_signal(barrier, inc=1, device_id={"cp": to}, device_id_type=MESH)
    pl.semaphore_wait(
        barrier, 1 + jnp.minimum(me // 2, 1) + jnp.minimum((n - 1 - me) // 2, 1))

    def fwd(kind, g, src_rows, dst_rows, to):
        return pltpu.make_async_remote_copy(
            src_ref=kv.at[g, :, src_rows], dst_ref=kv.at[g, :, dst_rows],
            send_sem=fs_sem.at[kind, g], recv_sem=fr_sem.at[kind, g],
            device_id={"cp": to}, device_id_type=MESH,
        )

    def fwd_x(g):
        return fwd(X, g, pl.ds((REACH - 2 * odd) * tok, tok), rows(1), partner)

    def fwd_b(g):
        return fwd(B, g, own_rows, rows(2), me + 2)

    def fwd_t(g):
        return fwd(T, g, rows(1), rows(3), me + 2)

    ahead = me + 2 < n
    behind = me >= 2
    x_in = is_odd | (me >= 2)
    x_out = is_even | (me >= 3)
    t_out = ahead & (me >= 1)
    t_in = me >= 3

    for g in range(heads):
        for c in kv_loads[g]:
            c.wait()
        @pl.when(ahead)
        def _():
            fwd_b(g).start()
        @pl.when(is_even)
        def _():
            fwd_x(g).start()

    for dist in range(1, REACH + 1):
        @pl.when(me < dist)
        def _():
            kv[:, :, (REACH - dist) * tok:(REACH - dist + 1) * tok, :] = jnp.zeros(
                (heads, 2, tok, HEAD), kv.dtype)

    window = (REACH + 1) * tok
    key_pos = (me - REACH) * tok + lax.broadcasted_iota(jnp.int32, (window, tok), 0)
    query_pos = me * tok + lax.broadcasted_iota(jnp.int32, (window, tok), 1)

    doc_load.wait()
    end = jnp.int32(0)
    crossed = jnp.zeros((window, tok), jnp.int32)
    def count(d, carry):
        end, crossed = carry
        end = end + doc_ref[d]
        return end, crossed + jnp.where((key_pos < end) & (query_pos >= end), 1, 0)
    if docs <= 8:
        for d in range(docs):
            end, crossed = count(d, (end, crossed))
    else:
        end, crossed = lax.fori_loop(0, docs, count, (end, crossed))
    allowed = (crossed == 0) & (key_pos <= query_pos) & (key_pos >= 0)
    bias[...] = jnp.where(allowed, 0.0, MASKED)

    def relay_x(g):
        @pl.when(behind)
        def _():
            fwd_b(g).wait_recv()
        @pl.when(is_odd & (me >= 3))
        def _():
            fwd_x(g).start()

    def relay_t(g):
        @pl.when(x_in)
        def _():
            fwd_x(g).wait_recv()
        @pl.when(t_out)
        def _():
            fwd_t(g).start()

    def arrive(g):
        @pl.when(t_in)
        def _():
            fwd_t(g).wait_recv()

    def bwd(kind, g, src_rows, to):
        return pltpu.make_async_remote_copy(
            src_ref=part.at[g, :, src_rows], dst_ref=back.at[kind, g],
            send_sem=bs_sem.at[kind, g], recv_sem=br_sem.at[kind, g],
            device_id={"cp": to}, device_id_type=MESH,
        )

    def bwd_x(g):
        return bwd(X, g, rows(1), partner)

    def bwd_b(g):
        return bwd(B, g, rows(2), me - 2)

    def bwd_t(g):
        return bwd(T, g, rows(3), me - 2)

    score_scale = 1.0 / math.sqrt(HEAD)
    exp_scale = score_scale * math.log2(math.e)
    nt = (((1,), (1,)), ((), ()))
    step = 2 if group % 2 == 0 else 1
    width = step * tok

    def compute(g):
        keys = kv[g, 0]
        values = kv[g, 1]
        keys_t = keys.T
        values_t = values.T
        grad_k = jnp.zeros((window, HEAD), jnp.float32)
        grad_v = jnp.zeros((window, HEAD), jnp.float32)
        mask = jnp.concatenate([bias[...]] * step, axis=1)
        for s in range(group // step):
            h0 = g * group + s * step
            for h in range(h0, h0 + step):
                for c in q_loads[h]:
                    c.wait()
            qs = qb[h0:h0 + step].reshape(width, HEAD)
            ds = db[h0:h0 + step].reshape(width, HEAD)
            scores = lax.dot_general(keys, qs, nt, preferred_element_type=jnp.float32) + mask
            top = jnp.max(scores, axis=0, keepdims=True)
            raw = jnp.exp2((scores - top) * exp_scale)
            probs = raw * (1.0 / jnp.sum(raw, axis=0, keepdims=True))
            low = probs.astype(jnp.bfloat16)
            att_t = jnp.dot(values_t, low, preferred_element_type=jnp.float32)
            grad_p = lax.dot_general(values, ds, nt, preferred_element_type=jnp.float32)
            delta = jnp.sum(probs * grad_p, axis=0, keepdims=True)
            grad_s = (probs * (grad_p - delta)).astype(jnp.bfloat16)
            grad_v = grad_v + jnp.dot(low, ds, preferred_element_type=jnp.float32)
            grad_k = grad_k + jnp.dot(grad_s, qs, preferred_element_type=jnp.float32)
            gq_t = jnp.dot(keys_t, grad_s, preferred_element_type=jnp.float32) * score_scale
            for j in range(step):
                h = h0 + j
                o_ref[:, cols(h)] = att_t[:, j * tok:(j + 1) * tok].T.astype(o_ref.dtype)
                gq_ref[:, cols(h)] = gq_t[:, j * tok:(j + 1) * tok].T.astype(gq_ref.dtype)
        for t, grad in enumerate((grad_k * score_scale, grad_v)):
            part[g, t] = grad[:REACH * tok].astype(part.dtype)
            mid[g, t] = grad[tok:REACH * tok]
            own[g, t] = grad[REACH * tok:]

    def back_t(g):
        @pl.when(t_in)
        def _():
            bwd_t(g).start()
        @pl.when(is_even & behind)
        def _():
            bwd_b(g).start()

    def back_x(g):
        @pl.when(t_out)
        def _():
            bwd_t(g).wait_recv()
            part[g, :, 2 * tok:] = (
                mid[g, :, tok:] + back[T, g].astype(jnp.float32)).astype(part.dtype)
        @pl.when(x_in)
        def _():
            bwd_x(g).start()

    def back_b(g):
        @pl.when(is_odd & (me >= 3))
        def _():
            bwd_x(g).wait_recv()
            part[g, :, tok:2 * tok] = (
                mid[g, :, :tok] + back[X, g].astype(jnp.float32)).astype(part.dtype)
            bwd_b(g).start()

    def finish(g):
        @pl.when(is_even)
        def _():
            bwd_x(g).wait_recv()
            own[g] = own[g] + back[X, g].astype(jnp.float32)
        @pl.when(ahead)
        def _():
            bwd_b(g).wait_recv()
            own[g] = own[g] + back[B, g].astype(jnp.float32)
        gk_ref[:, cols(g)] = own[g, 0].astype(gk_ref.dtype)
        gv_ref[:, cols(g)] = own[g, 1].astype(gv_ref.dtype)

    relay_x(0)
    if heads > 1:
        relay_x(1)
    relay_t(0)
    for g in range(heads + REACH):
        if g < heads:
            if g + 2 < heads:
                relay_x(g + 2)
            if g + 1 < heads:
                relay_t(g + 1)
            arrive(g)
            compute(g)
            back_t(g)
        for lag, stage in enumerate((back_x, back_b, finish)):
            if 0 <= g - 1 - lag < heads:
                stage(g - 1 - lag)

    for g in range(heads):
        for cond, copies in (
            (ahead, (fwd_b,)), (x_out, (fwd_x,)), (t_out, (fwd_t,)),
            (behind, (bwd_b,)), (x_in, (bwd_x,)), (t_in, (bwd_t,)),
        ):
            @pl.when(cond)
            def _():
                for f in copies:
                    f(g).wait_send()


def put_out(*refs):
    sems = refs[-1]
    copies = [
        pltpu.make_async_copy(refs[t], refs[4 + t], sems.at[t]) for t in range(4)
    ]
    for c in copies:
        c.start()
    for c in copies:
        c.wait()


def shards(doc_lengths, queries, key_states, value_head_states, out_grad):
    tok = queries.shape[0]
    heads = key_states.shape[1] // HEAD
    q_heads = queries.shape[1] // HEAD
    n = lax.axis_size("cp")
    window = (REACH + 1) * tok
    bf16, f32 = jnp.bfloat16, jnp.float32
    hbm_spec = pl.BlockSpec(memory_space=pltpu.HBM)
    any_spec = pl.BlockSpec(memory_space=pl.ANY)
    dma = pltpu.SemaphoreType.DMA
    args = [
        pltpu.with_memory_space_constraint(x, pltpu.HBM)
        for x in (doc_lengths, queries, key_states, value_head_states, out_grad)
    ]
    outs = pl.pallas_call(
        functools.partial(kernel, n, doc_lengths.shape[0]),
        out_shape=[
            jax.ShapeDtypeStruct(queries.shape, bf16),
            jax.ShapeDtypeStruct(queries.shape, bf16),
            jax.ShapeDtypeStruct(key_states.shape, bf16),
            jax.ShapeDtypeStruct(key_states.shape, bf16),
        ],
        in_specs=[hbm_spec] * 5,
        out_specs=[pl.BlockSpec(memory_space=pltpu.VMEM)] * 4,
        scratch_shapes=[
            pltpu.VMEM((heads, 2, window, HEAD), bf16),
            pltpu.VMEM((q_heads, tok, HEAD), bf16),
            pltpu.VMEM((q_heads, tok, HEAD), bf16),
            pltpu.VMEM((heads, 2, tok, HEAD), f32),
            pltpu.VMEM((heads, 2, 2 * tok, HEAD), f32),
            pltpu.VMEM((heads, 2, REACH * tok, HEAD), bf16),
            pltpu.VMEM((3, heads, 2, tok, HEAD), bf16),
            pltpu.VMEM((window, tok), f32),
            pltpu.SMEM(doc_lengths.shape, jnp.int32),
            dma(()),
            dma((heads, 2)),
            dma((2, q_heads)),
            dma((3, heads)),
            dma((3, heads)),
            dma((3, heads)),
            dma((3, heads)),
        ],
        compiler_params=pltpu.CompilerParams(
            collective_id=0, has_side_effects=True, vmem_limit_bytes=24 * 2**20),
        name="attend",
    )(*args)
    return tuple(pl.pallas_call(
        put_out,
        out_shape=[jax.ShapeDtypeStruct(x.shape, x.dtype) for x in outs],
        in_specs=[any_spec] * 4,
        out_specs=[hbm_spec] * 4,
        scratch_shapes=[dma((4,))],
        compiler_params=pltpu.CompilerParams(vmem_limit_bytes=2**20),
        name="put_out",
    )(*outs))


def solution(mesh):
    wide = P(("group", "cp"), "hd")
    return jax.shard_map(
        shards,
        mesh=mesh,
        in_specs=(P("group"), wide, wide, wide, wide),
        out_specs=(wide, wide, wide, wide),
        check_vma=False,
    )
```

profile of v0, /device:TPU:10, one launch (start us, length us, event | category | flops | bytes accessed | tf_op | source)
XLA Modules:
  0.0 36.8 jit_solution(2734564178575481527)
XLA Ops:
  0.6 35.1 %attend.1 = (bf16[128,2048]{1,0:T(8,128)(2,1)S(1)}, bf16[128,2048]{1,0:T(8,128)(2,1)S(1)}, bf16[128,512]{1,0:T(8,128)(2,1)S(1)}, bf16[128,512]{1,0:T(8,128)(2,1)S(1)}) custom-call(s32[4]{0:T(128)} %doc_hbm.1, bf16[128,2048]{1,0:T(8,128)(2,1)} %q_hbm.1, bf16[128,512]{1,0:T(8,128)(2,1)} %k_hbm.1, bf16[128,512]{1,0:T(8,128)(2,1)} %v_hbm.1, bf16[128,2048]{1,0:T(8,128)(2,1)} %do_hbm.1), custom_call_target="tpu_custom_call" | custom-call | tf_op jit(solution)/shard_map/attend/pallas_call | solution.py:294
  35.7 1.1 %put_out.1 = (bf16[128,2048]{1,0:T(8,128)(2,1)}, bf16[128,2048]{1,0:T(8,128)(2,1)}, bf16[128,512]{1,0:T(8,128)(2,1)}, bf16[128,512]{1,0:T(8,128)(2,1)}) custom-call(bf16[128,2048]{1,0:T(8,128)(2,1)S(1)} %get-tuple-element.8.refs_0_, bf16[128,2048]{1,0:T(8,128)(2,1)S(1)} %get-tuple-element.9.refs_1_, bf16[128,512]{1,0:T(8,128)(2,1)S(1)} %get-tuple-element.10.refs_2_, ...), custom_call_target="tpu_custom_call" | custom-call | tf_op jit(solution)/shard_map/put_out/pallas_call | solution.py:326
where the time goes:
time: 37.4 us; the launch traced here: 36.8 us
  Pallas kernels  36.1 us (97%)
  between operations  0.64 us (2%)
    pallas_call x1, Pallas kernels, shards(): pl.pallas_call(functools.partial(kernel, n, doc_lengths.shape[0]), out_sh...  35.1 us
    pallas_call x1, Pallas kernels, shards(): pl.pallas_call(put_out, out_shape=[jax.ShapeDtypeStruct(x.shape, x.dtype)...  1.08 us

commit v1 on v0

--- a/solution.py
+++ b/solution.py
@@ -161,40 +161,36 @@
     score_scale = 1.0 / math.sqrt(HEAD)
     exp_scale = score_scale * math.log2(math.e)
     nt = (((1,), (1,)), ((), ()))
-    step = 2 if group % 2 == 0 else 1
-    width = step * tok
+    width = group * tok
 
     def compute(g):
         keys = kv[g, 0]
         values = kv[g, 1]
         keys_t = keys.T
         values_t = values.T
-        grad_k = jnp.zeros((window, HEAD), jnp.float32)
-        grad_v = jnp.zeros((window, HEAD), jnp.float32)
-        mask = jnp.concatenate([bias[...]] * step, axis=1)
-        for s in range(group // step):
-            h0 = g * group + s * step
-            for h in range(h0, h0 + step):
-                for c in q_loads[h]:
-                    c.wait()
-            qs = qb[h0:h0 + step].reshape(width, HEAD)
-            ds = db[h0:h0 + step].reshape(width, HEAD)
-            scores = lax.dot_general(keys, qs, nt, preferred_element_type=jnp.float32) + mask
-            top = jnp.max(scores, axis=0, keepdims=True)
-            raw = jnp.exp2((scores - top) * exp_scale)
-            probs = raw * (1.0 / jnp.sum(raw, axis=0, keepdims=True))
-            low = probs.astype(jnp.bfloat16)
-            att_t = jnp.dot(values_t, low, preferred_element_type=jnp.float32)
-            grad_p = lax.dot_general(values, ds, nt, preferred_element_type=jnp.float32)
-            delta = jnp.sum(probs * grad_p, axis=0, keepdims=True)
-            grad_s = (probs * (grad_p - delta)).astype(jnp.bfloat16)
-            grad_v = grad_v + jnp.dot(low, ds, preferred_element_type=jnp.float32)
-            grad_k = grad_k + jnp.dot(grad_s, qs, preferred_element_type=jnp.float32)
-            gq_t = jnp.dot(keys_t, grad_s, preferred_element_type=jnp.float32) * score_scale
-            for j in range(step):
-                h = h0 + j
-                o_ref[:, cols(h)] = att_t[:, j * tok:(j + 1) * tok].T.astype(o_ref.dtype)
-                gq_ref[:, cols(h)] = gq_t[:, j * tok:(j + 1) * tok].T.astype(gq_ref.dtype)
+        mask = jnp.concatenate([bias[...]] * group, axis=1)
+        h0 = g * group
+        for h in range(h0, h0 + group):
+            for c in q_loads[h]:
+                c.wait()
+        qs = qb[h0:h0 + group].reshape(width, HEAD)
+        ds = db[h0:h0 + group].reshape(width, HEAD)
+        scores = lax.dot_general(keys, qs, nt, preferred_element_type=jnp.float32) + mask
+        top = jnp.max(scores, axis=0, keepdims=True)
+        raw = jnp.exp2((scores - top) * exp_scale)
+        probs = raw * (1.0 / jnp.sum(raw, axis=0, keepdims=True))
+        low = probs.astype(jnp.bfloat16)
+        att_t = jnp.dot(values_t, low, preferred_element_type=jnp.float32)
+        grad_p = lax.dot_general(values, ds, nt, preferred_element_type=jnp.float32)
+        delta = jnp.sum(probs * grad_p, axis=0, keepdims=True)
+        grad_s = (probs * (grad_p - delta)).astype(jnp.bfloat16)
+        grad_v = jnp.dot(low, ds, preferred_element_type=jnp.float32)
+        grad_k = jnp.dot(grad_s, qs, preferred_element_type=jnp.float32)
+        gq_t = jnp.dot(keys_t, grad_s, preferred_element_type=jnp.float32) * score_scale
+        for j in range(group):
+            h = h0 + j
+            o_ref[:, cols(h)] = att_t[:, j * tok:(j + 1) * tok].T.astype(o_ref.dtype)
+            gq_ref[:, cols(h)] = gq_t[:, j * tok:(j + 1) * tok].T.astype(gq_ref.dtype)
         for t, grad in enumerate((grad_k * score_scale, grad_v)):
             part[g, t] = grad[:REACH * tok].astype(part.dtype)
             mid[g, t] = grad[tok:REACH * tok]

time: 37.4 us -> 35.8 us (0.957)
  Pallas kernels: 36.1 us -> 34.9 us
    pallas_call x1, Pallas kernels: 35.1 us -> 33.8 us  [shards(): pl.pallas_call(functools.partial(kernel, n, doc_lengths.shape[0]), out_sh...]
where the time goes in v1:
time: 35.8 us; the launch traced here: 35.5 us
  Pallas kernels  34.9 us (97%)
  between operations  0.64 us (2%)
    pallas_call x1, Pallas kernels, shards(): pl.pallas_call(functools.partial(kernel, n, doc_lengths.shape[0]), out_sh...  33.8 us
    pallas_call x1, Pallas kernels, shards(): pl.pallas_call(put_out, out_shape=[jax.ShapeDtypeStruct(x.shape, x.dtype)...  1.08 us

profile of v1, /device:TPU:10, one launch (start us, length us, event | category | flops | bytes accessed | tf_op | source)
XLA Modules:
  0.0 35.5 jit_solution(17356809712715294318)
XLA Ops:
  0.6 33.8 %attend.1 = (bf16[128,2048]{1,0:T(8,128)(2,1)S(1)}, bf16[128,2048]{1,0:T(8,128)(2,1)S(1)}, bf16[128,512]{1,0:T(8,128)(2,1)S(1)}, bf16[128,512]{1,0:T(8,128)(2,1)S(1)}) custom-call(s32[4]{0:T(128)} %doc_hbm.1, bf16[128,2048]{1,0:T(8,128)(2,1)} %q_hbm.1, bf16[128,512]{1,0:T(8,128)(2,1)} %k_hbm.1, bf16[128,512]{1,0:T(8,128)(2,1)} %v_hbm.1, bf16[128,2048]{1,0:T(8,128)(2,1)} %do_hbm.1), custom_call_target="tpu_custom_call" | custom-call | tf_op jit(solution)/shard_map/attend/pallas_call | solution.py:290
  34.5 1.1 %put_out.1 = (bf16[128,2048]{1,0:T(8,128)(2,1)}, bf16[128,2048]{1,0:T(8,128)(2,1)}, bf16[128,512]{1,0:T(8,128)(2,1)}, bf16[128,512]{1,0:T(8,128)(2,1)}) custom-call(bf16[128,2048]{1,0:T(8,128)(2,1)S(1)} %get-tuple-element.8.refs_0_, bf16[128,2048]{1,0:T(8,128)(2,1)S(1)} %get-tuple-element.9.refs_1_, bf16[128,512]{1,0:T(8,128)(2,1)S(1)} %get-tuple-element.10.refs_2_, ...), custom_call_target="tpu_custom_call" | custom-call | tf_op jit(solution)/shard_map/put_out/pallas_call | solution.py:322

commit v2 on v1

--- a/solution.py
+++ b/solution.py
@@ -12,12 +12,12 @@
 REACH = 3
 MASKED = -1e30
 MESH = pl.DeviceIdType.MESH
-X, B, T = range(3)
+X, B, T, F = range(4)
 
 
 def kernel(
     n, docs, doc_hbm, q_hbm, k_hbm, v_hbm, do_hbm, o_ref, gq_ref, gk_ref, gv_ref,
-    kv, qb, db, own, mid, part, back, bias, doc_ref,
+    kv, qd, own, mid, part, back, bias, doc_ref,
     doc_sem, kv_sem, q_sem, fs_sem, fr_sem, bs_sem, br_sem,
 ):
     tok = q_hbm.shape[0]
@@ -46,38 +46,47 @@
         ])
         for c in kv_loads[g]:
             c.start()
-    q_loads = []
     for h in range(heads * group):
-        q_loads.append([
-            pltpu.make_async_copy(q_hbm.at[:, cols(h)], qb.at[h], q_sem.at[0, h]),
-            pltpu.make_async_copy(do_hbm.at[:, cols(h)], db.at[h], q_sem.at[1, h]),
-        ])
-        for c in q_loads[h]:
-            c.start()
+        for t, src in enumerate((q_hbm, do_hbm)):
+            pltpu.make_async_copy(
+                src.at[:, cols(h)], qd.at[t, h], q_sem.at[h // group]).start()
 
     barrier = pltpu.get_barrier_semaphore()
-    for to, cond in ((me - 2, me >= 2), (me + 2, me + 2 < n), (partner, me >= 0)):
+    across = me - 1 + 2 * odd
+    for to, cond in (
+        (me - 2, me >= 2), (me + 2, me + 2 < n), (partner, me >= 0),
+        (across, (across >= 1) & (across < n)),
+    ):
         @pl.when(cond)
         def _():
             pl.semaphore_signal(barrier, inc=1, device_id={"cp": to}, device_id_type=MESH)
     pl.semaphore_wait(
-        barrier, 1 + jnp.minimum(me // 2, 1) + jnp.minimum((n - 1 - me) // 2, 1))
-
-    def fwd(kind, g, src_rows, dst_rows, to):
+        barrier,
+        1 + jnp.minimum(me // 2, 1) + jnp.minimum((n - 1 - me) // 2, 1)
+        + jnp.where((across >= 1) & (across < n), 1, 0))
+
+
+    def fwd(kind, g, t, src_rows, dst_rows, to):
         return pltpu.make_async_remote_copy(
-            src_ref=kv.at[g, :, src_rows], dst_ref=kv.at[g, :, dst_rows],
-            send_sem=fs_sem.at[kind, g], recv_sem=fr_sem.at[kind, g],
+            src_ref=kv.at[g, t, src_rows], dst_ref=kv.at[g, t, dst_rows],
+            send_sem=fs_sem.at[kind], recv_sem=fr_sem.at[kind, g, t],
             device_id={"cp": to}, device_id_type=MESH,
         )
 
-    def fwd_x(g):
-        return fwd(X, g, pl.ds((REACH - 2 * odd) * tok, tok), rows(1), partner)
-
-    def fwd_b(g):
-        return fwd(B, g, own_rows, rows(2), me + 2)
-
-    def fwd_t(g):
-        return fwd(T, g, rows(1), rows(3), me + 2)
+    def drain(sem, block):
+        pltpu.make_async_remote_copy(
+            src_ref=block, dst_ref=block, send_sem=sem, recv_sem=fr_sem.at[X, 0, 0],
+            device_id={"cp": partner}, device_id_type=MESH,
+        ).wait_send()
+
+    def fwd_x(g, t):
+        return fwd(X, g, t, pl.ds((REACH - 2 * odd) * tok, tok), rows(1), partner)
+
+    def fwd_b(g, t):
+        return fwd(B, g, t, own_rows, rows(2), me + 2)
+
+    def fwd_t(g, t):
+        return fwd(T, g, t, rows(1), rows(3), me + 2)
 
     ahead = me + 2 < n
     behind = me >= 2
@@ -85,16 +94,17 @@
     x_out = is_even | (me >= 3)
     t_out = ahead & (me >= 1)
     t_in = me >= 3
-
-    for g in range(heads):
-        for c in kv_loads[g]:
-            c.wait()
+    parts = [(g, t) for g in range(heads) for t in range(2)]
+
+    last = heads - 1
+    for g, t in parts:
+        kv_loads[g][t].wait()
         @pl.when(ahead)
         def _():
-            fwd_b(g).start()
+            fwd_b(g, t).start()
         @pl.when(is_even)
         def _():
-            fwd_x(g).start()
+            fwd_x(g, t).start()
 
     for dist in range(1, REACH + 1):
         @pl.when(me < dist)
@@ -121,42 +131,54 @@
     allowed = (crossed == 0) & (key_pos <= query_pos) & (key_pos >= 0)
     bias[...] = jnp.where(allowed, 0.0, MASKED)
 
-    def relay_x(g):
+    def relay_x(g, t):
         @pl.when(behind)
         def _():
-            fwd_b(g).wait_recv()
+            fwd_b(g, t).wait_recv()
         @pl.when(is_odd & (me >= 3))
         def _():
-            fwd_x(g).start()
-
-    def relay_t(g):
-        @pl.when(x_in)
-        def _():
-            fwd_x(g).wait_recv()
-        @pl.when(t_out)
-        def _():
-            fwd_t(g).start()
+            fwd_x(g, t).start()
+
+    def x_arrive(g, t):
+        @pl.when(is_odd)
+        def _():
+            fwd_x(g, t).wait_recv()
+        @pl.when(is_odd & ahead)
+        def _():
+            fwd_t(g, t).start()
+
+    def relay_t(g, t):
+        @pl.when(is_even & behind)
+        def _():
+            fwd_x(g, t).wait_recv()
+        @pl.when(is_even & t_out)
+        def _():
+            fwd_t(g, t).start()
 
     def arrive(g):
         @pl.when(t_in)
         def _():
-            fwd_t(g).wait_recv()
-
-    def bwd(kind, g, src_rows, to):
+            for t in range(2):
+                fwd_t(g, t).wait_recv()
+
+    def bwd(kind, g, t, src_rows, to):
         return pltpu.make_async_remote_copy(
-            src_ref=part.at[g, :, src_rows], dst_ref=back.at[kind, g],
-            send_sem=bs_sem.at[kind, g], recv_sem=br_sem.at[kind, g],
+            src_ref=part.at[g, t, src_rows], dst_ref=back.at[kind, g, t],
+            send_sem=bs_sem.at[min(kind, T)], recv_sem=br_sem.at[kind, g, t],
             device_id={"cp": to}, device_id_type=MESH,
         )
 
-    def bwd_x(g):
-        return bwd(X, g, rows(1), partner)
-
-    def bwd_b(g):
-        return bwd(B, g, rows(2), me - 2)
-
-    def bwd_t(g):
-        return bwd(T, g, rows(3), me - 2)
+    def bwd_x(g, t):
+        return bwd(X, g, t, rows(1), partner)
+
+    def bwd_b(g, t):
+        return bwd(B, g, t, rows(2), me - 2)
+
+    def bwd_t(g, t):
+        return bwd(T, g, t, rows(3), me - 2)
+
+    def bwd_f(g, t):
+        return bwd(F, g, t, rows(3), me - 1)
 
     score_scale = 1.0 / math.sqrt(HEAD)
     exp_scale = score_scale * math.log2(math.e)
@@ -170,11 +192,10 @@
         values_t = values.T
         mask = jnp.concatenate([bias[...]] * group, axis=1)
         h0 = g * group
-        for h in range(h0, h0 + group):
-            for c in q_loads[h]:
-                c.wait()
-        qs = qb[h0:h0 + group].reshape(width, HEAD)
-        ds = db[h0:h0 + group].reshape(width, HEAD)
+        loaded = qd.at[:, h0:h0 + group]
+        pltpu.make_async_copy(loaded, loaded, q_sem.at[g]).wait()
+        qs = qd[0, h0:h0 + group].reshape(width, HEAD)
+        ds = qd[1, h0:h0 + group].reshape(width, HEAD)
         scores = lax.dot_general(keys, qs, nt, preferred_element_type=jnp.float32) + mask
         top = jnp.max(scores, axis=0, keepdims=True)
         raw = jnp.exp2((scores - top) * exp_scale)
@@ -196,70 +217,95 @@
             mid[g, t] = grad[tok:REACH * tok]
             own[g, t] = grad[REACH * tok:]
 
-    def back_t(g):
-        @pl.when(t_in)
-        def _():
-            bwd_t(g).start()
+    def back_start(g):
+        @pl.when(t_in & is_odd)
+        def _():
+            for t in range(2):
+                bwd_t(g, t).start()
+        @pl.when(t_in & is_even)
+        def _():
+            for t in range(2):
+                bwd_f(g, t).start()
         @pl.when(is_even & behind)
         def _():
-            bwd_b(g).start()
-
-    def back_x(g):
-        @pl.when(t_out)
-        def _():
-            bwd_t(g).wait_recv()
-            part[g, :, 2 * tok:] = (
-                mid[g, :, tok:] + back[T, g].astype(jnp.float32)).astype(part.dtype)
-        @pl.when(x_in)
-        def _():
-            bwd_x(g).start()
-
-    def back_b(g):
-        @pl.when(is_odd & (me >= 3))
-        def _():
-            bwd_x(g).wait_recv()
-            part[g, :, tok:2 * tok] = (
-                mid[g, :, :tok] + back[X, g].astype(jnp.float32)).astype(part.dtype)
-            bwd_b(g).start()
-
-    def finish(g):
+            for t in range(2):
+                bwd_x(g, t).start()
+            for t in range(2):
+                bwd_b(g, t).start()
+
+    def back_x(g, t):
+        @pl.when(is_odd & ahead)
+        def _():
+            bwd_t(g, t).wait_recv()
+            part[g, t, 2 * tok:] = (
+                mid[g, t, tok:] + back[T, g, t].astype(jnp.float32)).astype(part.dtype)
+        @pl.when(is_odd)
+        def _():
+            bwd_x(g, t).start()
+
+    def back_b(g, t):
+        passes = is_odd & (me >= 3)
+        @pl.when(passes)
+        def _():
+            bwd_x(g, t).wait_recv()
+            mid[g, t, :tok] = mid[g, t, :tok] + back[X, g, t].astype(jnp.float32)
+        far_in(g, t)
+        @pl.when(passes)
+        def _():
+            part[g, t, tok:2 * tok] = mid[g, t, :tok].astype(part.dtype)
+            bwd_b(g, t).start()
+
+    def far_in(g, t):
+        @pl.when(is_odd & (me >= 3) & (me + 1 < n))
+        def _():
+            bwd_f(g, t).wait_recv()
+            mid[g, t, :tok] = mid[g, t, :tok] + back[F, g, t].astype(jnp.float32)
+
+    def finish(g, t):
         @pl.when(is_even)
         def _():
-            bwd_x(g).wait_recv()
-            own[g] = own[g] + back[X, g].astype(jnp.float32)
+            bwd_x(g, t).wait_recv()
+            own[g, t] = own[g, t] + back[X, g, t].astype(jnp.float32)
         @pl.when(ahead)
         def _():
-            bwd_b(g).wait_recv()
-            own[g] = own[g] + back[B, g].astype(jnp.float32)
-        gk_ref[:, cols(g)] = own[g, 0].astype(gk_ref.dtype)
-        gv_ref[:, cols(g)] = own[g, 1].astype(gv_ref.dtype)
-
-    relay_x(0)
-    if heads > 1:
-        relay_x(1)
-    relay_t(0)
-    for g in range(heads + REACH):
-        if g < heads:
-            if g + 2 < heads:
-                relay_x(g + 2)
-            if g + 1 < heads:
-                relay_t(g + 1)
-            arrive(g)
-            compute(g)
-            back_t(g)
-        for lag, stage in enumerate((back_x, back_b, finish)):
-            if 0 <= g - 1 - lag < heads:
-                stage(g - 1 - lag)
-
+            bwd_b(g, t).wait_recv()
+            own[g, t] = own[g, t] + back[B, g, t].astype(jnp.float32)
+        out = gv_ref if t else gk_ref
+        out[:, cols(g)] = own[g, t].astype(out.dtype)
+
+    for g, t in parts:
+        relay_x(g, t)
+        x_arrive(g, t)
+    for g, t in parts[:-2]:
+        relay_t(g, t)
     for g in range(heads):
-        for cond, copies in (
-            (ahead, (fwd_b,)), (x_out, (fwd_x,)), (t_out, (fwd_t,)),
-            (behind, (bwd_b,)), (x_in, (bwd_x,)), (t_in, (bwd_t,)),
-        ):
-            @pl.when(cond)
-            def _():
-                for f in copies:
-                    f(g).wait_send()
+        arrive(g)
+        compute(g)
+        back_start(g)
+        if g == 0:
+            for t in range(2):
+                relay_t(last, t)
+    lag = 2
+    for g in range(heads + lag):
+        for t in range(2):
+            if g < heads:
+                back_x(g, t)
+            if g >= lag:
+                back_b(g - lag, t)
+    for g, t in parts:
+        finish(g, t)
+
+    for cond, sem, block in (
+        (ahead, fs_sem.at[B], kv.at[:, :, own_rows]),
+        (x_out, fs_sem.at[X], kv.at[:, :, own_rows]),
+        (t_out, fs_sem.at[T], kv.at[:, :, own_rows]),
+        (behind, bs_sem.at[B], kv.at[:, :, own_rows]),
+        (x_in, bs_sem.at[X], kv.at[:, :, own_rows]),
+        (t_in, bs_sem.at[T], kv.at[:, :, own_rows]),
+    ):
+        @pl.when(cond)
+        def _():
+            drain(sem, block)
 
 
 def put_out(*refs):
@@ -299,21 +345,20 @@
         out_specs=[pl.BlockSpec(memory_space=pltpu.VMEM)] * 4,
         scratch_shapes=[
             pltpu.VMEM((heads, 2, window, HEAD), bf16),
-            pltpu.VMEM((q_heads, tok, HEAD), bf16),
-            pltpu.VMEM((q_heads, tok, HEAD), bf16),
+            pltpu.VMEM((2, q_heads, tok, HEAD), bf16),
             pltpu.VMEM((heads, 2, tok, HEAD), f32),
             pltpu.VMEM((heads, 2, 2 * tok, HEAD), f32),
             pltpu.VMEM((heads, 2, REACH * tok, HEAD), bf16),
-            pltpu.VMEM((3, heads, 2, tok, HEAD), bf16),
+            pltpu.VMEM((4, heads, 2, tok, HEAD), bf16),
             pltpu.VMEM((window, tok), f32),
             pltpu.SMEM(doc_lengths.shape, jnp.int32),
             dma(()),
             dma((heads, 2)),
-            dma((2, q_heads)),
-            dma((3, heads)),
-            dma((3, heads)),
-            dma((3, heads)),
-            dma((3, heads)),
+            dma((heads,)),
+            dma((3,)),
+            dma((3, heads, 2)),
+            dma((3,)),
+            dma((4, heads, 2)),
         ],
         compiler_params=pltpu.CompilerParams(
             collective_id=0, has_side_effects=True, vmem_limit_bytes=24 * 2**20),

time: 35.8 us -> 30.1 us (0.84)
  Pallas kernels: 34.9 us -> 29.3 us
    pallas_call x1, Pallas kernels: 33.8 us -> 28.2 us  [shards(): pl.pallas_call(functools.partial(kernel, n, doc_lengths.shape[0]), out_sh...]
where the time goes in v2:
time: 30.1 us; the launch traced here: 30 us
  Pallas kernels  29.3 us (97%)
  between operations  0.64 us (2%)
    pallas_call x1, Pallas kernels, shards(): pl.pallas_call(functools.partial(kernel, n, doc_lengths.shape[0]), out_sh...  28.2 us
    pallas_call x1, Pallas kernels, shards(): pl.pallas_call(put_out, out_shape=[jax.ShapeDtypeStruct(x.shape, x.dtype)...  1.08 us

profile of v2, /device:TPU:10, one launch (start us, length us, event | category | flops | bytes accessed | tf_op | source)
XLA Modules:
  0.0 30.0 jit_solution(7210339373273440128)
XLA Ops:
  0.6 28.2 %attend.1 = (bf16[128,2048]{1,0:T(8,128)(2,1)S(1)}, bf16[128,2048]{1,0:T(8,128)(2,1)S(1)}, bf16[128,512]{1,0:T(8,128)(2,1)S(1)}, bf16[128,512]{1,0:T(8,128)(2,1)S(1)}) custom-call(s32[4]{0:T(128)} %doc_hbm.1, bf16[128,2048]{1,0:T(8,128)(2,1)} %q_hbm.1, bf16[128,512]{1,0:T(8,128)(2,1)} %k_hbm.1, bf16[128,512]{1,0:T(8,128)(2,1)} %v_hbm.1, bf16[128,2048]{1,0:T(8,128)(2,1)} %do_hbm.1), custom_call_target="tpu_custom_call" | custom-call | tf_op jit(solution)/shard_map/attend/pallas_call | solution.py:336
  28.9 1.1 %put_out.1 = (bf16[128,2048]{1,0:T(8,128)(2,1)}, bf16[128,2048]{1,0:T(8,128)(2,1)}, bf16[128,512]{1,0:T(8,128)(2,1)}, bf16[128,512]{1,0:T(8,128)(2,1)}) custom-call(bf16[128,2048]{1,0:T(8,128)(2,1)S(1)} %get-tuple-element.8.refs_0_, bf16[128,2048]{1,0:T(8,128)(2,1)S(1)} %get-tuple-element.9.refs_1_, bf16[128,512]{1,0:T(8,128)(2,1)S(1)} %get-tuple-element.10.refs_2_, ...), custom_call_target="tpu_custom_call" | custom-call | tf_op jit(solution)/shard_map/put_out/pallas_call | solution.py:367

commit v3 on v2

--- a/solution.py
+++ b/solution.py
@@ -17,7 +17,7 @@
 
 def kernel(
     n, docs, doc_hbm, q_hbm, k_hbm, v_hbm, do_hbm, o_ref, gq_ref, gk_ref, gv_ref,
-    kv, qd, own, mid, part, back, bias, doc_ref,
+    kv, qd, own, mid, part, back, low_ref, grad_ref, bias, doc_ref,
     doc_sem, kv_sem, q_sem, fs_sem, fr_sem, bs_sem, br_sem,
 ):
     tok = q_hbm.shape[0]
@@ -28,6 +28,8 @@
     is_odd = odd == 1
     is_even = odd == 0
     partner = me + 1 - 2 * odd
+    short = lax.axis_index("hd") == 0
+    slow = is_odd | jnp.logical_not(short)
     own_rows = pl.ds(REACH * tok, tok)
 
     def rows(dist):
@@ -97,14 +99,19 @@
     parts = [(g, t) for g in range(heads) for t in range(2)]
 
     last = heads - 1
-    for g, t in parts:
+    early = 4
+
+    def send_own(cond, g, t):
+        @pl.when(cond & ahead)
+        def _():
+            fwd_b(g, t).start()
+        @pl.when(cond & is_even)
+        def _():
+            fwd_x(g, t).start()
+
+    for i, (g, t) in enumerate(parts):
         kv_loads[g][t].wait()
-        @pl.when(ahead)
-        def _():
-            fwd_b(g, t).start()
-        @pl.when(is_even)
-        def _():
-            fwd_x(g, t).start()
+        send_own(short if i >= early else me >= 0, g, t)
 
     for dist in range(1, REACH + 1):
         @pl.when(me < dist)
@@ -147,11 +154,11 @@
         def _():
             fwd_t(g, t).start()
 
-    def relay_t(g, t):
-        @pl.when(is_even & behind)
+    def relay_t(g, t, now):
+        @pl.when(now & is_even & behind)
         def _():
             fwd_x(g, t).wait_recv()
-        @pl.when(is_even & t_out)
+        @pl.when(now & is_even & t_out)
         def _():
             fwd_t(g, t).start()
 
@@ -185,61 +192,63 @@
     nt = (((1,), (1,)), ((), ()))
     width = group * tok
 
+    def cotangents(t, g):
+        return qd[t, g * group:(g + 1) * group].reshape(width, HEAD)
+
     def compute(g):
         keys = kv[g, 0]
         values = kv[g, 1]
-        keys_t = keys.T
-        values_t = values.T
         mask = jnp.concatenate([bias[...]] * group, axis=1)
-        h0 = g * group
-        loaded = qd.at[:, h0:h0 + group]
+        loaded = qd.at[:, g * group:(g + 1) * group]
         pltpu.make_async_copy(loaded, loaded, q_sem.at[g]).wait()
-        qs = qd[0, h0:h0 + group].reshape(width, HEAD)
-        ds = qd[1, h0:h0 + group].reshape(width, HEAD)
+        qs = cotangents(0, g)
+        ds = cotangents(1, g)
         scores = lax.dot_general(keys, qs, nt, preferred_element_type=jnp.float32) + mask
         top = jnp.max(scores, axis=0, keepdims=True)
         raw = jnp.exp2((scores - top) * exp_scale)
         probs = raw * (1.0 / jnp.sum(raw, axis=0, keepdims=True))
         low = probs.astype(jnp.bfloat16)
-        att_t = jnp.dot(values_t, low, preferred_element_type=jnp.float32)
+        low_ref[g] = low
         grad_p = lax.dot_general(values, ds, nt, preferred_element_type=jnp.float32)
         delta = jnp.sum(probs * grad_p, axis=0, keepdims=True)
         grad_s = (probs * (grad_p - delta)).astype(jnp.bfloat16)
+        grad_ref[g] = grad_s
         grad_v = jnp.dot(low, ds, preferred_element_type=jnp.float32)
         grad_k = jnp.dot(grad_s, qs, preferred_element_type=jnp.float32)
-        gq_t = jnp.dot(keys_t, grad_s, preferred_element_type=jnp.float32) * score_scale
-        for j in range(group):
-            h = h0 + j
-            o_ref[:, cols(h)] = att_t[:, j * tok:(j + 1) * tok].T.astype(o_ref.dtype)
-            gq_ref[:, cols(h)] = gq_t[:, j * tok:(j + 1) * tok].T.astype(gq_ref.dtype)
         for t, grad in enumerate((grad_k * score_scale, grad_v)):
             part[g, t] = grad[:REACH * tok].astype(part.dtype)
             mid[g, t] = grad[tok:REACH * tok]
             own[g, t] = grad[REACH * tok:]
 
+    def outputs(g):
+        for t, weights, out, scale in ((1, low_ref, o_ref, 1.0), (0, grad_ref, gq_ref, score_scale)):
+            res = jnp.dot(kv[g, t].T, weights[g], preferred_element_type=jnp.float32) * scale
+            for j in range(group):
+                out[:, cols(g * group + j)] = (
+                    res[:, j * tok:(j + 1) * tok].T.astype(out.dtype))
+
     def back_start(g):
-        @pl.when(t_in & is_odd)
-        def _():
-            for t in range(2):
-                bwd_t(g, t).start()
-        @pl.when(t_in & is_even)
-        def _():
-            for t in range(2):
-                bwd_f(g, t).start()
-        @pl.when(is_even & behind)
-        def _():
-            for t in range(2):
-                bwd_x(g, t).start()
-            for t in range(2):
+        for cond, f in (
+            (t_in & slow, bwd_t), (t_in & is_even & short, bwd_f), (is_even & behind & short, bwd_x),
+        ):
+            @pl.when(cond)
+            def _():
+                for t in range(2):
+                    f(g, t).start()
+
+    def back_even(cond):
+        @pl.when(is_even & behind & cond)
+        def _():
+            for g, t in parts:
                 bwd_b(g, t).start()
 
-    def back_x(g, t):
-        @pl.when(is_odd & ahead)
+    def back_x(g, t, now):
+        @pl.when(now & slow & t_out)
         def _():
             bwd_t(g, t).wait_recv()
             part[g, t, 2 * tok:] = (
                 mid[g, t, tok:] + back[T, g, t].astype(jnp.float32)).astype(part.dtype)
-        @pl.when(is_odd)
+        @pl.when(now & slow & x_in)
         def _():
             bwd_x(g, t).start()
 
@@ -256,7 +265,7 @@
             bwd_b(g, t).start()
 
     def far_in(g, t):
-        @pl.when(is_odd & (me >= 3) & (me + 1 < n))
+        @pl.when(is_odd & (me >= 3) & (me + 1 < n) & short)
         def _():
             bwd_f(g, t).wait_recv()
             mid[g, t, :tok] = mid[g, t, :tok] + back[F, g, t].astype(jnp.float32)
@@ -273,25 +282,40 @@
         out = gv_ref if t else gk_ref
         out[:, cols(g)] = own[g, t].astype(out.dtype)
 
-    for g, t in parts:
+    for i, (g, t) in enumerate(parts):
         relay_x(g, t)
+        if i + early < len(parts):
+            send_own(jnp.logical_not(short), *parts[i + early])
         x_arrive(g, t)
     for g, t in parts[:-2]:
-        relay_t(g, t)
+        relay_t(g, t, me >= 0)
     for g in range(heads):
         arrive(g)
         compute(g)
         back_start(g)
-        if g == 0:
-            for t in range(2):
-                relay_t(last, t)
-    lag = 2
-    for g in range(heads + lag):
+        for when, core in ((0, short), (min(1, last), jnp.logical_not(short))):
+            if g == when:
+                for t in range(2):
+                    relay_t(last, t, core)
+    back_even(short)
+    ahead_of = 2 if heads > 1 else 1
+    for h in range(heads):
         for t in range(2):
-            if g < heads:
-                back_x(g, t)
-            if g >= lag:
-                back_b(g - lag, t)
+            back_x(h, t, me >= 0)
+        if h == 0:
+            for g in range(ahead_of):
+                outputs(g)
+            continue
+        for t in range(2):
+            back_b(h - 1, t)
+        if h + 1 < heads:
+            outputs(h + 1)
+        if h + 2 == heads:
+            back_even(jnp.logical_not(short))
+    if heads < 2:
+        back_even(jnp.logical_not(short))
+    for t in range(2):
+        back_b(last, t)
     for g, t in parts:
         finish(g, t)
 
@@ -350,6 +374,8 @@
             pltpu.VMEM((heads, 2, 2 * tok, HEAD), f32),
             pltpu.VMEM((heads, 2, REACH * tok, HEAD), bf16),
             pltpu.VMEM((4, heads, 2, tok, HEAD), bf16),
+            pltpu.VMEM((heads, window, q_heads // heads * tok), bf16),
+            pltpu.VMEM((heads, window, q_heads // heads * tok), bf16),
             pltpu.VMEM((window, tok), f32),
             pltpu.SMEM(doc_lengths.shape, jnp.int32),
             dma(()),

time: 30.1 us -> 29.5 us (0.980)
  the two profiles are of different devices: /device:TPU:10 before, /device:TPU:11 now
where the time goes in v3:
time: 29.5 us; the launch traced here: 29.3 us
  Pallas kernels  28.6 us (97%)
  between operations  0.64 us (2%)
    pallas_call x1, Pallas kernels, shards(): pl.pallas_call(functools.partial(kernel, n, doc_lengths.shape[0]), out_sh...  27.5 us
    pallas_call x1, Pallas kernels, shards(): pl.pallas_call(put_out, out_shape=[jax.ShapeDtypeStruct(x.shape, x.dtype)...  1.08 us

profile of v3, /device:TPU:11, one launch (start us, length us, event | category | flops | bytes accessed | tf_op | source)
XLA Modules:
  0.0 29.3 jit_solution(3694093629034413309)
XLA Ops:
  0.6 27.5 %attend.1 = (bf16[128,2048]{1,0:T(8,128)(2,1)S(1)}, bf16[128,2048]{1,0:T(8,128)(2,1)S(1)}, bf16[128,512]{1,0:T(8,128)(2,1)S(1)}, bf16[128,512]{1,0:T(8,128)(2,1)S(1)}) custom-call(s32[4]{0:T(128)} %doc_hbm.1, bf16[128,2048]{1,0:T(8,128)(2,1)} %q_hbm.1, bf16[128,512]{1,0:T(8,128)(2,1)} %k_hbm.1, bf16[128,512]{1,0:T(8,128)(2,1)} %v_hbm.1, bf16[128,2048]{1,0:T(8,128)(2,1)} %do_hbm.1), custom_call_target="tpu_custom_call" | custom-call | tf_op jit(solution)/shard_map/attend/pallas_call | solution.py:360
  28.2 1.1 %put_out.1 = (bf16[128,2048]{1,0:T(8,128)(2,1)}, bf16[128,2048]{1,0:T(8,128)(2,1)}, bf16[128,512]{1,0:T(8,128)(2,1)}, bf16[128,512]{1,0:T(8,128)(2,1)}) custom-call(bf16[128,2048]{1,0:T(8,128)(2,1)S(1)} %get-tuple-element.8.refs_0_, bf16[128,2048]{1,0:T(8,128)(2,1)S(1)} %get-tuple-element.9.refs_1_, bf16[128,512]{1,0:T(8,128)(2,1)S(1)} %get-tuple-element.10.refs_2_, ...), custom_call_target="tpu_custom_call" | custom-call | tf_op jit(solution)/shard_map/put_out/pallas_call | solution.py:393

commit v4 on v3

--- a/solution.py
+++ b/solution.py
@@ -12,7 +12,7 @@
 REACH = 3
 MASKED = -1e30
 MESH = pl.DeviceIdType.MESH
-X, B, T, F = range(4)
+X, B, T = range(3)
 
 
 def kernel(
@@ -29,7 +29,6 @@
     is_even = odd == 0
     partner = me + 1 - 2 * odd
     short = lax.axis_index("hd") == 0
-    slow = is_odd | jnp.logical_not(short)
     own_rows = pl.ds(REACH * tok, tok)
 
     def rows(dist):
@@ -54,18 +53,13 @@
                 src.at[:, cols(h)], qd.at[t, h], q_sem.at[h // group]).start()
 
     barrier = pltpu.get_barrier_semaphore()
-    across = me - 1 + 2 * odd
-    for to, cond in (
-        (me - 2, me >= 2), (me + 2, me + 2 < n), (partner, me >= 0),
-        (across, (across >= 1) & (across < n)),
-    ):
+    for to, cond in ((me - 2, me >= 2), (me + 2, me + 2 < n), (partner, me >= 0)):
         @pl.when(cond)
         def _():
             pl.semaphore_signal(barrier, inc=1, device_id={"cp": to}, device_id_type=MESH)
     pl.semaphore_wait(
         barrier,
-        1 + jnp.minimum(me // 2, 1) + jnp.minimum((n - 1 - me) // 2, 1)
-        + jnp.where((across >= 1) & (across < n), 1, 0))
+        1 + jnp.minimum(me // 2, 1) + jnp.minimum((n - 1 - me) // 2, 1))
 
 
     def fwd(kind, g, t, src_rows, dst_rows, to):
@@ -97,6 +91,7 @@
     t_out = ahead & (me >= 1)
     t_in = me >= 3
     parts = [(g, t) for g in range(heads) for t in range(2)]
+    turned = [(g, 1 - t) for g, t in parts]
 
     last = heads - 1
     early = 4
@@ -171,7 +166,7 @@
     def bwd(kind, g, t, src_rows, to):
         return pltpu.make_async_remote_copy(
             src_ref=part.at[g, t, src_rows], dst_ref=back.at[kind, g, t],
-            send_sem=bs_sem.at[min(kind, T)], recv_sem=br_sem.at[kind, g, t],
+            send_sem=bs_sem.at[kind], recv_sem=br_sem.at[kind, g, t],
             device_id={"cp": to}, device_id_type=MESH,
         )
 
@@ -183,9 +178,6 @@
 
     def bwd_t(g, t):
         return bwd(T, g, t, rows(3), me - 2)
-
-    def bwd_f(g, t):
-        return bwd(F, g, t, rows(3), me - 1)
 
     score_scale = 1.0 / math.sqrt(HEAD)
     exp_scale = score_scale * math.log2(math.e)
@@ -209,16 +201,19 @@
         probs = raw * (1.0 / jnp.sum(raw, axis=0, keepdims=True))
         low = probs.astype(jnp.bfloat16)
         low_ref[g] = low
+        keep(g, 1, jnp.dot(low, ds, preferred_element_type=jnp.float32))
+        back_start(g, 1)
         grad_p = lax.dot_general(values, ds, nt, preferred_element_type=jnp.float32)
         delta = jnp.sum(probs * grad_p, axis=0, keepdims=True)
         grad_s = (probs * (grad_p - delta)).astype(jnp.bfloat16)
         grad_ref[g] = grad_s
-        grad_v = jnp.dot(low, ds, preferred_element_type=jnp.float32)
-        grad_k = jnp.dot(grad_s, qs, preferred_element_type=jnp.float32)
-        for t, grad in enumerate((grad_k * score_scale, grad_v)):
-            part[g, t] = grad[:REACH * tok].astype(part.dtype)
-            mid[g, t] = grad[tok:REACH * tok]
-            own[g, t] = grad[REACH * tok:]
+        keep(g, 0, jnp.dot(grad_s, qs, preferred_element_type=jnp.float32) * score_scale)
+        back_start(g, 0)
+
+    def keep(g, t, grad):
+        part[g, t] = grad[:REACH * tok].astype(part.dtype)
+        mid[g, t] = grad[tok:REACH * tok]
+        own[g, t] = grad[REACH * tok:]
 
     def outputs(g):
         for t, weights, out, scale in ((1, low_ref, o_ref, 1.0), (0, grad_ref, gq_ref, score_scale)):
@@ -227,48 +222,34 @@
                 out[:, cols(g * group + j)] = (
                     res[:, j * tok:(j + 1) * tok].T.astype(out.dtype))
 
-    def back_start(g):
-        for cond, f in (
-            (t_in & slow, bwd_t), (t_in & is_even & short, bwd_f), (is_even & behind & short, bwd_x),
-        ):
-            @pl.when(cond)
-            def _():
-                for t in range(2):
-                    f(g, t).start()
+    def back_start(g, t):
+        @pl.when(t_in)
+        def _():
+            bwd_t(g, t).start()
 
     def back_even(cond):
         @pl.when(is_even & behind & cond)
         def _():
-            for g, t in parts:
+            for g, t in turned:
                 bwd_b(g, t).start()
 
-    def back_x(g, t, now):
-        @pl.when(now & slow & t_out)
+    def back_x(g, t):
+        @pl.when(t_out)
         def _():
             bwd_t(g, t).wait_recv()
             part[g, t, 2 * tok:] = (
                 mid[g, t, tok:] + back[T, g, t].astype(jnp.float32)).astype(part.dtype)
-        @pl.when(now & slow & x_in)
+        @pl.when(x_in)
         def _():
             bwd_x(g, t).start()
 
     def back_b(g, t):
-        passes = is_odd & (me >= 3)
-        @pl.when(passes)
+        @pl.when(is_odd & (me >= 3))
         def _():
             bwd_x(g, t).wait_recv()
-            mid[g, t, :tok] = mid[g, t, :tok] + back[X, g, t].astype(jnp.float32)
-        far_in(g, t)
-        @pl.when(passes)
-        def _():
-            part[g, t, tok:2 * tok] = mid[g, t, :tok].astype(part.dtype)
+            part[g, t, tok:2 * tok] = (
+                mid[g, t, :tok] + back[X, g, t].astype(jnp.float32)).astype(part.dtype)
             bwd_b(g, t).start()
-
-    def far_in(g, t):
-        @pl.when(is_odd & (me >= 3) & (me + 1 < n) & short)
-        def _():
-            bwd_f(g, t).wait_recv()
-            mid[g, t, :tok] = mid[g, t, :tok] + back[F, g, t].astype(jnp.float32)
 
     def finish(g, t):
         @pl.when(is_even)
@@ -292,31 +273,19 @@
     for g in range(heads):
         arrive(g)
         compute(g)
-        back_start(g)
         for when, core in ((0, short), (min(1, last), jnp.logical_not(short))):
             if g == when:
                 for t in range(2):
                     relay_t(last, t, core)
     back_even(short)
-    ahead_of = 2 if heads > 1 else 1
     for h in range(heads):
-        for t in range(2):
-            back_x(h, t, me >= 0)
-        if h == 0:
-            for g in range(ahead_of):
-                outputs(g)
-            continue
-        for t in range(2):
-            back_b(h - 1, t)
-        if h + 1 < heads:
-            outputs(h + 1)
-        if h + 2 == heads:
-            back_even(jnp.logical_not(short))
-    if heads < 2:
-        back_even(jnp.logical_not(short))
-    for t in range(2):
-        back_b(last, t)
-    for g, t in parts:
+        for t in (1, 0):
+            back_x(h, t)
+        outputs(h)
+    back_even(jnp.logical_not(short))
+    for g, t in turned:
+        back_b(g, t)
+    for g, t in turned:
         finish(g, t)
 
     for cond, sem, block in (
@@ -373,7 +342,7 @@
             pltpu.VMEM((heads, 2, tok, HEAD), f32),
             pltpu.VMEM((heads, 2, 2 * tok, HEAD), f32),
             pltpu.VMEM((heads, 2, REACH * tok, HEAD), bf16),
-            pltpu.VMEM((4, heads, 2, tok, HEAD), bf16),
+            pltpu.VMEM((3, heads, 2, tok, HEAD), bf16),
             pltpu.VMEM((heads, window, q_heads // heads * tok), bf16),
             pltpu.VMEM((heads, window, q_heads // heads * tok), bf16),
             pltpu.VMEM((window, tok), f32),
@@ -384,7 +353,7 @@
             dma((3,)),
             dma((3, heads, 2)),
             dma((3,)),
-            dma((4, heads, 2)),
+            dma((3, heads, 2)),
         ],
         compiler_params=pltpu.CompilerParams(
             collective_id=0, has_side_effects=True, vmem_limit_bytes=24 * 2**20),

time: 29.5 us -> 29 us (0.983)
  the two profiles are of different devices: /device:TPU:11 before, /device:TPU:10 now
where the time goes in v4:
time: 29 us; the launch traced here: 28.8 us
  Pallas kernels  28.2 us (97%)
  between operations  0.64 us (2%)
    pallas_call x1, Pallas kernels, shards(): pl.pallas_call(functools.partial(kernel, n, doc_lengths.shape[0]), out_sh...  27.1 us
    pallas_call x1, Pallas kernels, shards(): pl.pallas_call(put_out, out_shape=[jax.ShapeDtypeStruct(x.shape, x.dtype)...  1.08 us

profile of v4, /device:TPU:10, one launch (start us, length us, event | category | flops | bytes accessed | tf_op | source)
XLA Modules:
  0.0 28.8 jit_solution(11767175523400715205)
XLA Ops:
  0.6 27.1 %attend.1 = (bf16[128,2048]{1,0:T(8,128)(2,1)S(1)}, bf16[128,2048]{1,0:T(8,128)(2,1)S(1)}, bf16[128,512]{1,0:T(8,128)(2,1)S(1)}, bf16[128,512]{1,0:T(8,128)(2,1)S(1)}) custom-call(s32[4]{0:T(128)} %doc_hbm.1, bf16[128,2048]{1,0:T(8,128)(2,1)} %q_hbm.1, bf16[128,512]{1,0:T(8,128)(2,1)} %k_hbm.1, bf16[128,512]{1,0:T(8,128)(2,1)} %v_hbm.1, bf16[128,2048]{1,0:T(8,128)(2,1)} %do_hbm.1), custom_call_target="tpu_custom_call" | custom-call | tf_op jit(solution)/shard_map/attend/pallas_call | solution.py:329
  27.7 1.1 %put_out.1 = (bf16[128,2048]{1,0:T(8,128)(2,1)}, bf16[128,2048]{1,0:T(8,128)(2,1)}, bf16[128,512]{1,0:T(8,128)(2,1)}, bf16[128,512]{1,0:T(8,128)(2,1)}) custom-call(bf16[128,2048]{1,0:T(8,128)(2,1)S(1)} %get-tuple-element.8.refs_0_, bf16[128,2048]{1,0:T(8,128)(2,1)S(1)} %get-tuple-element.9.refs_1_, bf16[128,512]{1,0:T(8,128)(2,1)S(1)} %get-tuple-element.10.refs_2_, ...), custom_call_target="tpu_custom_call" | custom-call | tf_op jit(solution)/shard_map/put_out/pallas_call | solution.py:362

commit v5 on v4

--- a/solution.py
+++ b/solution.py
@@ -17,7 +17,7 @@
 
 def kernel(
     n, docs, doc_hbm, q_hbm, k_hbm, v_hbm, do_hbm, o_ref, gq_ref, gk_ref, gv_ref,
-    kv, qd, own, mid, part, back, low_ref, grad_ref, bias, doc_ref,
+    kv, qd, own, mid, part, back, low_ref, grad_ref, bias, near, doc_ref,
     doc_sem, kv_sem, q_sem, fs_sem, fr_sem, bs_sem, br_sem,
 ):
     tok = q_hbm.shape[0]
@@ -131,7 +131,12 @@
     else:
         end, crossed = lax.fori_loop(0, docs, count, (end, crossed))
     allowed = (crossed == 0) & (key_pos <= query_pos) & (key_pos >= 0)
-    bias[...] = jnp.where(allowed, 0.0, MASKED)
+    full = jnp.where(allowed, 0.0, MASKED)
+    mine = (lax.broadcasted_iota(jnp.int32, (tok, tok), 0)
+            <= lax.broadcasted_iota(jnp.int32, (tok, tok), 1))
+    bias[:tok] = jnp.where(mine, full[REACH * tok:], full[:tok])
+    bias[tok:] = full[tok:REACH * tok]
+    near[...] = jnp.where(mine, 1.0, 0.0).astype(near.dtype)
 
     def relay_x(g, t):
         @pl.when(behind)
@@ -191,21 +196,32 @@
         keys = kv[g, 0]
         values = kv[g, 1]
         mask = jnp.concatenate([bias[...]] * group, axis=1)
+        near_low = jnp.concatenate([near[...]] * group, axis=1)
+        nearer = jnp.concatenate([mine] * group, axis=1)
+
+        def join(x):
+            return jnp.concatenate(
+                [jnp.where(nearer, x[REACH * tok:], x[:tok]), x[tok:REACH * tok]], axis=0)
+
+        def split(x):
+            own_part = x[:tok] * near_low
+            return jnp.concatenate([x[:tok] - own_part, x[tok:], own_part], axis=0)
+
         loaded = qd.at[:, g * group:(g + 1) * group]
         pltpu.make_async_copy(loaded, loaded, q_sem.at[g]).wait()
         qs = cotangents(0, g)
         ds = cotangents(1, g)
-        scores = lax.dot_general(keys, qs, nt, preferred_element_type=jnp.float32) + mask
+        scores = join(lax.dot_general(keys, qs, nt, preferred_element_type=jnp.float32)) + mask
         top = jnp.max(scores, axis=0, keepdims=True)
         raw = jnp.exp2((scores - top) * exp_scale)
         probs = raw * (1.0 / jnp.sum(raw, axis=0, keepdims=True))
-        low = probs.astype(jnp.bfloat16)
+        low = split(probs.astype(jnp.bfloat16))
         low_ref[g] = low
         keep(g, 1, jnp.dot(low, ds, preferred_element_type=jnp.float32))
         back_start(g, 1)
-        grad_p = lax.dot_general(values, ds, nt, preferred_element_type=jnp.float32)
+        grad_p = join(lax.dot_general(values, ds, nt, preferred_element_type=jnp.float32))
         delta = jnp.sum(probs * grad_p, axis=0, keepdims=True)
-        grad_s = (probs * (grad_p - delta)).astype(jnp.bfloat16)
+        grad_s = split((probs * (grad_p - delta)).astype(jnp.bfloat16))
         grad_ref[g] = grad_s
         keep(g, 0, jnp.dot(grad_s, qs, preferred_element_type=jnp.float32) * score_scale)
         back_start(g, 0)
@@ -345,7 +361,8 @@
             pltpu.VMEM((3, heads, 2, tok, HEAD), bf16),
             pltpu.VMEM((heads, window, q_heads // heads * tok), bf16),
             pltpu.VMEM((heads, window, q_heads // heads * tok), bf16),
-            pltpu.VMEM((window, tok), f32),
+            pltpu.VMEM((REACH * tok, tok), f32),
+            pltpu.VMEM((tok, tok), bf16),
             pltpu.SMEM(doc_lengths.shape, jnp.int32),
             dma(()),
             dma((heads, 2)),

time: 29 us -> 28.8 us (level)
  Pallas kernels: 28.2 us -> 27.9 us
where the time goes in v5:
time: 28.8 us; the launch traced here: 28.6 us
  Pallas kernels  27.9 us (97%)
  between operations  0.64 us (2%)
    pallas_call x1, Pallas kernels, shards(): pl.pallas_call(functools.partial(kernel, n, doc_lengths.shape[0]), out_sh...  26.9 us
    pallas_call x1, Pallas kernels, shards(): pl.pallas_call(put_out, out_shape=[jax.ShapeDtypeStruct(x.shape, x.dtype)...  1.08 us

profile of v5, /device:TPU:10, one launch (start us, length us, event | category | flops | bytes accessed | tf_op | source)
XLA Modules:
  0.0 28.6 jit_solution(5324715013751391898)
XLA Ops:
  0.6 26.9 %attend.1 = (bf16[128,2048]{1,0:T(8,128)(2,1)S(1)}, bf16[128,2048]{1,0:T(8,128)(2,1)S(1)}, bf16[128,512]{1,0:T(8,128)(2,1)S(1)}, bf16[128,512]{1,0:T(8,128)(2,1)S(1)}) custom-call(s32[4]{0:T(128)} %doc_hbm.1, bf16[128,2048]{1,0:T(8,128)(2,1)} %q_hbm.1, bf16[128,512]{1,0:T(8,128)(2,1)} %k_hbm.1, bf16[128,512]{1,0:T(8,128)(2,1)} %v_hbm.1, bf16[128,2048]{1,0:T(8,128)(2,1)} %do_hbm.1), custom_call_target="tpu_custom_call" | custom-call | tf_op jit(solution)/shard_map/attend/pallas_call | solution.py:345
  27.5 1.1 %put_out.1 = (bf16[128,2048]{1,0:T(8,128)(2,1)}, bf16[128,2048]{1,0:T(8,128)(2,1)}, bf16[128,512]{1,0:T(8,128)(2,1)}, bf16[128,512]{1,0:T(8,128)(2,1)}) custom-call(bf16[128,2048]{1,0:T(8,128)(2,1)S(1)} %get-tuple-element.8.refs_0_, bf16[128,2048]{1,0:T(8,128)(2,1)S(1)} %get-tuple-element.9.refs_1_, bf16[128,512]{1,0:T(8,128)(2,1)S(1)} %get-tuple-element.10.refs_2_, ...), custom_call_target="tpu_custom_call" | custom-call | tf_op jit(solution)/shard_map/put_out/pallas_call | solution.py:379
